TPU v7x, 32 devices: a whole 2x2x4 slice. The times are simulated.
32 devices in a mesh: cuts: 8 (over z, x), mode: 4 (over y, core).
Axes of the slice: x: 2, y: 2, z: 4, core: 2. Of those that a mesh axis runs over, the one named last changes fastest.
Arguments:
- sliced_state: bfloat16 [8, 16, 4, 128, 2, 128], P(None, 'cuts', None, 'mode'), may hold values from -0.75 to 0.75
- gate_blocks: bfloat16 [32, 2, 128, 128], P('cuts'), may hold values from -0.375 to 0.375
- gate_slot: int32 [32], replicated, may hold values from 0 to 31, each once
- samples: int32 [8, 4096], replicated, may hold values from 0 to 65535
Outputs:
- amplitudes: float32 [32, 128, 2, 128], P('cuts', 'mode')
- sample_probs: float32 [8, 4096], replicated
- xeb_score: float32 [8], replicated
Inputs may be any that keep to these rules, and one draw needn't show every extreme that they name: `gate_slot`: a permutation: every gate block has its own row of gate_blocks. `samples`: flat index s * 128 * 128 + p * 128 + q.
All inputs are finite; a program needn't handle non-finite values.
Results may differ from a plain program's by a relative error of at most 0.022.
Values may be sent and summed in bfloat16 or wider, within the bound.
A program may use at most 64 MiB of HBM per device.

v0:
```python
import jax
import jax.numpy as jnp
from jax import lax
from jax.sharding import PartitionSpec as P


def from_root(array, axis, root):
    mine = lax.axis_index(axis) == root
    return lax.psum(jnp.where(mine, array, jnp.zeros_like(array)), axis)


def apply_gates(tensor, blocks):
    real_part = blocks[:, 0]
    imag_part = blocks[:, 1]
    stacked = jnp.concatenate(
        [
            jnp.concatenate([real_part, imag_part], axis=2),
            jnp.concatenate([-imag_part, real_part], axis=2),
        ],
        axis=1,
    )
    layout = tensor.shape
    flattened = tensor.reshape(layout[0], -1, 2 * layout[-1])
    product = jnp.einsum("crk,ckn->crn", flattened, stacked, preferred_element_type=jnp.float32)
    return product.astype(jnp.bfloat16).reshape(layout)


def select_rows(table, wanted):
    count = table.shape[0]
    onehot = (wanted[:, None] == jnp.arange(count, dtype=jnp.int32)[None, :]).astype(table.dtype)
    picked = jnp.dot(onehot, table.reshape(count, -1), preferred_element_type=jnp.float32)
    return picked.astype(table.dtype).reshape((wanted.shape[0],) + table.shape[1:])


def on_device(sliced_state, gate_blocks, gate_slot, samples):
    circuits = sliced_state.shape[0]
    spectator = sliced_state.shape[2]
    width = sliced_state.shape[5]
    held_count = gate_blocks.shape[0]
    layer_count = gate_slot.shape[0] // (2 * circuits)
    circuit_ids = jnp.arange(circuits, dtype=jnp.int32)
    tensor = lax.all_to_all(sliced_state, "mode", split_axis=0, concat_axis=3, tiled=True)
    local_count = tensor.shape[0]
    local_ids = lax.axis_index("mode") * local_count + jnp.arange(local_count, dtype=jnp.int32)

    def fetch_one(position):
        held_block = select_rows(gate_blocks, jnp.reshape(position % held_count, (1,)))[0]
        return from_root(held_block, "cuts", position // held_count)

    def fetch_gates(layer_index, gate_kind):
        fetched = []
        for circuit in range(local_count):
            fetched.append(
                fetch_one(
                    gate_slot[(local_ids[circuit] * layer_count + layer_index) * 2 + gate_kind]
                )
            )
        return jnp.stack(fetched, axis=0)

    for layer_index in range(layer_count):
        tensor = apply_gates(tensor, fetch_gates(layer_index, 0))
        tensor = jnp.swapaxes(tensor, 3, 5)
        tensor = apply_gates(tensor, fetch_gates(layer_index, 1))
        tensor = jnp.swapaxes(tensor, 3, 5)
    summed = jnp.sum(tensor.astype(jnp.float32), axis=1)
    summed = lax.all_to_all(
        summed.astype(jnp.bfloat16), "mode", split_axis=2, concat_axis=0, tiled=True
    ).astype(summed.dtype)
    local_rows = summed.shape[2]
    summed = summed.reshape(circuits * spectator, local_rows, 2, width)
    amplitudes = lax.psum_scatter(
        summed.astype(jnp.bfloat16), "cuts", scatter_dimension=0, tiled=True
    ).astype(jnp.float32)
    row_count = amplitudes.shape[0]
    first_row = lax.axis_index("cuts") * row_count
    first_col = lax.axis_index("mode") * local_rows
    magnitude = amplitudes[:, :, 0, :] ** 2 + amplitudes[:, :, 1, :] ** 2
    row_sums = jnp.sum(magnitude, axis=(1, 2))
    owner_circuit = (first_row + jnp.arange(row_count, dtype=jnp.int32)) // spectator
    norm_part = jnp.sum(
        jnp.where(owner_circuit[None, :] == circuit_ids[:, None], row_sums[None, :], 0.0), axis=1
    )
    plane_size = width * width
    spec_index = samples // plane_size
    row_index = samples // width % width
    col_index = samples % width
    local_row = circuit_ids[:, None] * spectator + spec_index - first_row
    local_col = row_index - first_col
    is_owned = (
        (local_row >= 0) & (local_row < row_count) & (local_col >= 0) & (local_col < local_rows)
    )
    cell_index = jnp.where(is_owned, local_row * local_rows + local_col, -1)
    cell_count = row_count * local_rows
    cell_onehot = (
        cell_index[:, :, None] == jnp.arange(cell_count, dtype=jnp.int32)[None, None, :]
    ).astype(jnp.float32)
    picked_rows = jnp.einsum(
        "csr,rw->csw",
        cell_onehot,
        magnitude.reshape(cell_count, width),
        precision=lax.Precision.HIGHEST,
    )
    col_match = col_index[:, :, None] == jnp.arange(width, dtype=jnp.int32)[None, None, :]
    sample_mass = jnp.sum(jnp.where(col_match, picked_rows, 0.0), axis=2)
    dimension_scale = float(spectator * plane_size)
    norm_total = lax.psum(norm_part, ("cuts", "mode"))
    sample_probs = lax.psum(sample_mass * dimension_scale / norm_total[:, None], ("cuts", "mode"))
    xeb_score = jnp.mean(sample_probs, axis=1)
    return (amplitudes, sample_probs, xeb_score)


def solution(mesh):
    in_specs = (P(None, "cuts", None, "mode", None, None), P("cuts", None, None, None), P(), P())
    out_specs = (P("cuts", "mode", None, None), P(), P())
    return jax.shard_map(
        on_device, mesh=mesh, in_specs=in_specs, out_specs=out_specs, check_vma=False
    )
```

profile of v0, /device:TPU:0, one launch (start us, length us, event | category | flops | bytes accessed | tf_op | source)
XLA Modules:
  0.0 402.5 jit_solution(14701239896464762398)
XLA Ops:
  7.2 0.6 fusion.74
  10.4 1.6 fusion.73
  32.4 1.2 copy.56
  33.9 0.7 copy.39
  35.0 0.7 copy.40
  37.7 0.6 convert_select_fusion.5
  38.3 0.6 convert_select_fusion.4
  39.0 0.6 convert_select_fusion.3
  39.6 0.6 convert_select_fusion.2
  40.2 0.6 convert_select_fusion.1
  40.8 0.6 convert_select_fusion
  41.5 4.3 %all-to-all-start = ((bf16[8,2,4,32,2,128]{5,4,3,2,1,0:T(2,128)(2,1)}), bf16[8,2,4,32,2,128]{5,4,3,2,1,0:T(2,128)(2,1)S(1)}, u32[]{:S(2)}, u32[]{:S(2)}) async-start(bf16[8,2,4,32,2,128]{5,4,3,2,1,0:T(2,128)(2,1)} %param.4), calls=%async_computation | async-start | bytes 2097152 | tf_op jit(solution)/shard_map/all_to_all | solution.py:42
  45.8 72.8 %all-reduce.6.cloned.1.call-done = (bf16[1,2,128,128]{2,3,0,1:T(8,128)(2,1)}, bf16[1,2,128,128]{2,3,0,1:T(8,128)(2,1)}, bf16[1,2,128,128]{3,2,0,1:T(8,128)(2,1)}...) async-done(((bf16[1,2,128,128]{2,3,0,1:T(8,128)(2,1)}, ...) | async-done | bytes 524304 | tf_op jit(solution)/shard_map/psum | solution.py:9
  118.6 0.9 constant_dynamic-update-slice_fusion.1
  119.5 0.9 constant_dynamic-update-slice_fusion
  120.4 0.8 constant_dynamic-update-slice_fusion.3
  121.2 0.8 constant_dynamic-update-slice_fusion.5
  122.1 0.9 constant_dynamic-update-slice_fusion.2
  123.1 1.2 copy.55
  124.4 0.7 reshape.305
  125.1 0.5 fusion.2
  125.5 0.8 reshape.306
  126.3 1.1 copy.42
  127.4 0.7 reshape.307
  128.1 0.4 convolution_convert_fusion.2
  128.6 0.3 reshape.308
  128.9 1.2 copy.43
  130.1 0.7 reshape.309
  130.8 0.4 convolution_convert_fusion.1
  131.2 0.3 reshape.310
  131.5 1.2 copy.44
  132.8 0.7 reshape.311
  133.5 0.4 convolution_convert_fusion
  133.9 0.3 reshape.312
  134.2 2.4 reduce_sum.50
  136.7 0.7 copy.45
  137.4 11.4 %all_to_all.33 = bf16[2,4,128,2,128]{4,3,1,0,2:T(2,128)(2,1)S(1)} all-to-all(bf16[2,4,128,2,128]{4,3,1,0,2:T(2,128)(2,1)S(1)} %copy.45), channel_id=1, replica_groups=mesh['cuts'=8,'mode'=4] {'mode'}, dimensions={2} | all-to-all | bytes 1048576 | tf_op jit(solution)/shard_map/all_to_all | solution.py:66
  148.9 0.8 copy.47
  149.9 61.7 %reduce-scatter.2.cloned.1.call-done = bf16[4,32,2,128]{3,1,2,0:T(8,128)(2,1)} async-done(((bf16[32,32,2,128]{3,1,2,0:T(8,128)(2,1)}), bf16[4,32,2,128]{3,1,2,0:T(8,128)(2,1)}) %reduce-scatter.2.cloned.1.call-update) | async-done | bytes 65552 | tf_op jit(solution)/shard_map/reduce_scatter | solution.py:71
  211.5 0.8 convert_element_type.77
  212.9 40.1 %psum.78 = f32[8]{0:T(128)S(1)} all-reduce(f32[8]{0:T(128)S(1)} %select_reduce_fusion.1), channel_id=1, replica_groups=mesh['cuts'=8,'mode'=4] {'cuts','mode'}, use_global_device_ids=true, to_apply=%region_13.14 | all-reduce | flops 8 | bytes 64 | tf_op jit(solution)/shard_map/psum | solution.py:106
  252.9 15.4 %select_reduce_fusion = f32[8,4096]{1,0:T(8,128)S(1)} fusion(s32[8,4096]{1,0:T(8,128)S(1)} %get-tuple-element.23, f32[128,128,1]{1,0,2:T(8,128)S(1)} %bitcast.154, s32[8,4096]{1,0:T(8,128)S(1)} %get-tuple-element.22), kind=kOutput, calls=%fused_computation | convolution fusion | flops 6459195392 | bytes 458752 | tf_op jit(solution)/shard_map/csr,rw->csw/dot_general | solution.py:97
  268.4 0.7 multiply_divide_fusion
  269.2 0.7 copy.49
  269.9 123.0 %all-reduce.4.cloned.1.call-done = f32[8,4096]{1,0:T(8,128)} async-done(((f32[8,4096]{1,0:T(8,128)}), f32[8,4096]{1,0:T(8,128)}) %all-reduce.4.cloned.1.call-update) | async-done | bytes 131088 | tf_op jit(solution)/shard_map/psum | solution.py:107
  392.8 1.1 reduce_sum.55
  393.9 0.5 broadcast_multiply_fusion
  394.4 1.6 copy.70
  (42 shorter events, 3.2 us)
Async XLA Ops:
  7.2 111.4 %all-reduce.6.cloned.1.call-start = ((), (), s32[]{:S(2)}) async-start(), calls=%async_computation.5 | async-start | bytes 1048576 | tf_op jit(solution)/shard_map/psum | solution.py:9
  41.5 81.6 %all-to-all-start = ((bf16[8,2,4,32,2,128]{5,4,3,2,1,0:T(2,128)(2,1)}), bf16[8,2,4,32,2,128]{5,4,3,2,1,0:T(2,128)(2,1)S(1)}, u32[]{:S(2)}, u32[]{:S(2)}) async-start(bf16[8,2,4,32,2,128]{5,4,3,2,1,0:T(2,128)(2,1)} %param.4), calls=%async_computation | async-start | bytes 2097152 | tf_op jit(solution)/shard_map/all_to_all | solution.py:42
  45.8 165.8 %reduce-scatter.2.cloned.1.call-start = ((), (), s32[]{:S(2)}) async-start(), calls=%async_computation.3 | async-start | bytes 589824 | tf_op jit(solution)/shard_map/reduce_scatter | solution.py:71
  118.6 4.4 %copy-start.3 = (bf16[1,2,128,128]{3,2,0,1:T(8,128)(2,1)S(1)}, bf16[1,2,128,128]{3,2,0,1:T(8,128)(2,1)}, u32[]{:S(2)}) copy-start(bf16[1,2,128,128]{3,2,0,1:T(8,128)(2,1)} %get-tuple-element.18) | copy-start | bytes 196612
  118.6 4.4 %copy-start.2 = (bf16[1,2,128,128]{3,2,0,1:T(8,128)(2,1)S(1)}, bf16[1,2,128,128]{3,2,0,1:T(8,128)(2,1)}, u32[]{:S(2)}) copy-start(bf16[1,2,128,128]{3,2,0,1:T(8,128)(2,1)} %get-tuple-element.19) | copy-start | bytes 196612
  148.9 63.7 %copy-start.1 = (s32[8,4096]{1,0:T(8,128)S(1)}, s32[8,4096]{1,0:T(8,128)}, u32[]{:S(2)}) copy-start(s32[8,4096]{1,0:T(8,128)} %param.7) | copy-start | bytes 393220
  149.8 243.0 %all-reduce.4.cloned.1.call-start = ((), (), s32[]{:S(2)}) async-start(), calls=%async_computation.4 | async-start | bytes 262144 | tf_op jit(solution)/shard_map/psum | solution.py:107
  252.9 16.2 %copy-start = (bf16[4,32,2,128]{3,1,2,0:T(8,128)(2,1)S(1)}, bf16[4,32,2,128]{3,1,2,0:T(8,128)(2,1)}, u32[]{:S(2)}) copy-start(bf16[4,32,2,128]{3,1,2,0:T(8,128)(2,1)} %reduce-scatter.2.cloned.1.call-done) | copy-start | bytes 196612
Sparse Core Ops, SparseCore 0:
  41.6 76.9 all-reduce.5
  149.9 61.5 reduce-scatter.1
  269.3 123.5 all-reduce.3
where the time goes:
time: 403 us; the launch traced here: 402 us
  waiting for transfers between devices  257 us (64%)
  blocking collectives  51.4 us (13%)
  between operations  37.4 us (9%)
  local copies, waits for them, and re-layouts  22.5 us (6%)
  matrix products  19.5 us (5%)
  other arithmetic  9.91 us (2%)
  starting transfers between devices  4.36 us (1%)
    psum x1, waiting for transfers between devices, on_device(): lax.psum(sample_mass * dimension_scale / norm_total[:, None], ('cuts', 'm...  123 us
    psum x1, waiting for transfers between devices, from_root(): return lax.psum(jnp.where(mine, array, jnp.zeros_like(array)), axis)  72.8 us
    reduce_scatter x1, waiting for transfers between devices, on_device(): lax.psum_scatter(summed.astype(jnp.bfloat16), 'cuts', scatter_dimension=0...  61.7 us
    psum x1, blocking collectives, on_device(): norm_total = lax.psum(norm_part, ('cuts', 'mode'))  40.1 us
    dot_general x1, matrix products, on_device(): jnp.einsum('csr,rw->csw', cell_onehot, magnitude.reshape(cell_count, widt...  15.4 us
    all_to_all x1, blocking collectives, on_device(): lax.all_to_all(summed.astype(jnp.bfloat16), 'mode', split_axis=2, concat_...  11.4 us
  transfers between devices with their start and end apart: 4, of which 3 were waited for; matrix products, arithmetic and copies ran while one was open for 1% of the time, Pallas kernels for 0%

commit v1 on v0

--- a/solution.py
+++ b/solution.py
@@ -4,9 +4,14 @@
 from jax.sharding import PartitionSpec as P
 
 
+def fill_area(field, mesh_ax):
+    e_next = jnp.sum(lax.all_gather(field, mesh_ax), 0)
+    return e_next
+
+
 def from_root(array, axis, root):
     mine = lax.axis_index(axis) == root
-    return lax.psum(jnp.where(mine, array, jnp.zeros_like(array)), axis)
+    return fill_area(jnp.where(mine, array, jnp.zeros_like(array)), axis)
 
 
 def apply_gates(tensor, blocks):

time: 403 us -> 575 us (1.43)
  blocking collectives: 51.4 us -> 304 us
  waiting for transfers between devices: 257 us -> 187 us
  local copies, waits for them, and re-layouts: 22.5 us -> 14.9 us
    all_gather x0 -> x8, blocking collectives: none -> 252 us  [fill_area(): e_next = jnp.sum(lax.all_gather(field, mesh_ax), 0)]
    psum x1 -> x0, waiting for transfers between devices: 72.8 us -> none  [from_root(): return lax.psum(jnp.where(mine, array, jnp.zeros_like(array)), axis)]
  transfers between devices with their start and end apart: 4 -> 3, of which waited for: 3 -> 2; matrix products, arithmetic and copies ran while one was open for 1% -> 1% of each run, Pallas kernels for 0% -> 0%
where the time goes in v1:
time: 575 us; the launch traced here: 574 us
  blocking collectives  304 us (53%)
  waiting for transfers between devices  187 us (33%)
  between operations  37.8 us (7%)
  matrix products  19.5 us (3%)
  local copies, waits for them, and re-layouts  14.9 us (3%)
  other arithmetic  6.86 us (1%)
    all_gather x8, blocking collectives, fill_area(): e_next = jnp.sum(lax.all_gather(field, mesh_ax), 0)  252 us
    psum x1, waiting for transfers between devices, on_device(): lax.psum(sample_mass * dimension_scale / norm_total[:, None], ('cuts', 'm...  123 us
    reduce_scatter x1, waiting for transfers between devices, on_device(): lax.psum_scatter(summed.astype(jnp.bfloat16), 'cuts', scatter_dimension=0...  63.6 us
    psum x1, blocking collectives, on_device(): norm_total = lax.psum(norm_part, ('cuts', 'mode'))  40.1 us
    dot_general x1, matrix products, on_device(): jnp.einsum('csr,rw->csw', cell_onehot, magnitude.reshape(cell_count, widt...  15.4 us
    all_to_all x1, blocking collectives, on_device(): lax.all_to_all(summed.astype(jnp.bfloat16), 'mode', split_axis=2, concat_...  11.8 us
  transfers between devices with their start and end apart: 3, of which 2 were waited for; matrix products, arithmetic and copies ran while one was open for 1% of the time, Pallas kernels for 0%

profile of v1, /device:TPU:0, one launch (start us, length us, event | category | flops | bytes accessed | tf_op | source)
XLA Modules:
  0.0 574.0 jit_solution(6343461777723463144)
XLA Ops:
  7.2 4.4 all-to-all-start
  11.6 0.6 fusion.90
  14.8 0.7 fusion.89
  36.1 0.3 fusion.51
  36.4 32.6 %all_gather.32 = bf16[8,2,128,128]{3,2,1,0:T(8,128)(2,1)S(1)} all-gather(bf16[1,2,128,128]{3,2,1,0:T(8,128)(2,1)S(1)} %bitcast.149), channel_id=1, replica_groups=mesh['cuts'=8,'mode'=4] {'cuts'}, dimensions={0}, use_global_device_ids=true | all-gather | bytes 589824 | tf_op jit(solution)/shard_map/all_gather | solution.py:8
  69.3 0.3 fusion.52
  69.6 31.5 %all_gather.33 = bf16[8,2,128,128]{3,2,1,0:T(8,128)(2,1)S(1)} all-gather(bf16[1,2,128,128]{3,2,1,0:T(8,128)(2,1)S(1)} %bitcast.150), channel_id=1, replica_groups=mesh['cuts'=8,'mode'=4] {'cuts'}, dimensions={0}, use_global_device_ids=true | all-gather | bytes 589824 | tf_op jit(solution)/shard_map/all_gather | solution.py:8
  101.3 0.3 fusion.53
  101.6 31.4 %all_gather.34 = bf16[8,2,128,128]{3,2,1,0:T(8,128)(2,1)S(1)} all-gather(bf16[1,2,128,128]{3,2,1,0:T(8,128)(2,1)S(1)} %bitcast.151), channel_id=1, replica_groups=mesh['cuts'=8,'mode'=4] {'cuts'}, dimensions={0}, use_global_device_ids=true | all-gather | bytes 589824 | tf_op jit(solution)/shard_map/all_gather | solution.py:8
  133.1 0.3 fusion.54
  133.4 31.2 %all_gather.35 = bf16[8,2,128,128]{3,2,1,0:T(8,128)(2,1)S(1)} all-gather(bf16[1,2,128,128]{3,2,1,0:T(8,128)(2,1)S(1)} %bitcast.152), channel_id=1, replica_groups=mesh['cuts'=8,'mode'=4] {'cuts'}, dimensions={0}, use_global_device_ids=true | all-gather | bytes 589824 | tf_op jit(solution)/shard_map/all_gather | solution.py:8
  164.7 0.3 fusion.55
  165.0 31.5 %all_gather.36 = bf16[8,2,128,128]{3,2,1,0:T(8,128)(2,1)S(1)} all-gather(bf16[1,2,128,128]{3,2,1,0:T(8,128)(2,1)S(1)} %bitcast.153), channel_id=1, replica_groups=mesh['cuts'=8,'mode'=4] {'cuts'}, dimensions={0}, use_global_device_ids=true | all-gather | bytes 589824 | tf_op jit(solution)/shard_map/all_gather | solution.py:8
  196.6 0.3 fusion.56
  196.9 31.3 %all_gather.37 = bf16[8,2,128,128]{3,2,1,0:T(8,128)(2,1)S(1)} all-gather(bf16[1,2,128,128]{3,2,1,0:T(8,128)(2,1)S(1)} %bitcast.154), channel_id=1, replica_groups=mesh['cuts'=8,'mode'=4] {'cuts'}, dimensions={0}, use_global_device_ids=true | all-gather | bytes 589824 | tf_op jit(solution)/shard_map/all_gather | solution.py:8
  228.3 0.3 fusion.57
  228.6 31.4 %all_gather.38 = bf16[8,2,128,128]{3,2,1,0:T(8,128)(2,1)S(1)} all-gather(bf16[1,2,128,128]{3,2,1,0:T(8,128)(2,1)S(1)} %bitcast.155), channel_id=1, replica_groups=mesh['cuts'=8,'mode'=4] {'cuts'}, dimensions={0}, use_global_device_ids=true | all-gather | bytes 589824 | tf_op jit(solution)/shard_map/all_gather | solution.py:8
  260.4 31.4 %all_gather.39 = bf16[8,2,128,128]{3,2,1,0:T(8,128)(2,1)S(1)} all-gather(bf16[1,2,128,128]{3,2,1,0:T(8,128)(2,1)S(1)} %bitcast.156), channel_id=1, replica_groups=mesh['cuts'=8,'mode'=4] {'cuts'}, dimensions={0}, use_global_device_ids=true | all-gather | bytes 589824 | tf_op jit(solution)/shard_map/all_gather | solution.py:8
  292.0 1.2 copy.60
  293.2 0.7 reshape.385
  293.9 0.5 fusion.2
  294.4 0.8 reshape.386
  295.2 1.1 copy.47
  296.3 0.7 reshape.387
  297.0 0.4 convolution_convert_fusion.2
  297.4 0.3 reshape.388
  297.7 1.2 copy.48
  298.9 0.7 reshape.389
  299.7 0.4 convolution_convert_fusion.1
  300.1 0.3 reshape.390
  300.4 1.2 copy.49
  301.6 0.7 reshape.391
  302.4 0.4 convolution_convert_fusion
  302.8 0.3 reshape.392
  303.1 2.4 reduce_sum.154
  305.5 0.7 copy.50
  306.3 11.8 %all_to_all.33 = bf16[2,4,128,2,128]{4,3,1,0,2:T(2,128)(2,1)S(1)} all-to-all(bf16[2,4,128,2,128]{4,3,1,0,2:T(2,128)(2,1)S(1)} %copy.50), channel_id=1, replica_groups=mesh['cuts'=8,'mode'=4] {'mode'}, dimensions={2} | all-to-all | bytes 1048576 | tf_op jit(solution)/shard_map/all_to_all | solution.py:71
  318.2 0.9 copy.52
  319.2 63.6 %reduce-scatter.2.cloned.1.call-done = bf16[4,32,2,128]{3,1,2,0:T(8,128)(2,1)} async-done(((bf16[32,32,2,128]{3,1,2,0:T(8,128)(2,1)}), bf16[4,32,2,128]{3,1,2,0:T(8,128)(2,1)}) %reduce-scatter.2.cloned.1.call-update) | async-done | bytes 65552 | tf_op jit(solution)/shard_map/reduce_scatter | solution.py:76
  382.8 0.8 convert_element_type.93
  384.1 40.1 %psum.14 = f32[8]{0:T(128)S(1)} all-reduce(f32[8]{0:T(128)S(1)} %select_reduce_fusion.1), channel_id=1, replica_groups=mesh['cuts'=8,'mode'=4] {'cuts','mode'}, use_global_device_ids=true, to_apply=%region_13.14 | all-reduce | flops 8 | bytes 64 | tf_op jit(solution)/shard_map/psum | solution.py:111
  424.2 15.4 %select_reduce_fusion = f32[8,4096]{1,0:T(8,128)S(1)} fusion(s32[8,4096]{1,0:T(8,128)S(1)} %get-tuple-element.26, f32[128,128,1]{1,0,2:T(8,128)S(1)} %bitcast.174, s32[8,4096]{1,0:T(8,128)S(1)} %get-tuple-element.25), kind=kOutput, calls=%fused_computation | convolution fusion | flops 6459195392 | bytes 458752 | tf_op jit(solution)/shard_map/csr,rw->csw/dot_general | solution.py:102
  439.6 0.7 multiply_divide_fusion
  440.4 0.7 copy.54
  441.1 122.9 %all-reduce.2.cloned.1.call-done = f32[8,4096]{1,0:T(8,128)} async-done(((f32[8,4096]{1,0:T(8,128)}), f32[8,4096]{1,0:T(8,128)}) %all-reduce.2.cloned.1.call-update) | async-done | bytes 131088 | tf_op jit(solution)/shard_map/psum | solution.py:112
  564.0 1.1 reduce_sum.159
  565.1 0.5 broadcast_multiply_fusion
  565.6 1.6 copy.63
  (48 shorter events, 2.2 us)
Async XLA Ops:
  7.2 7.7 %copy-start.3 = (s32[32]{0:T(128)S(1)}, s32[32]{0:T(128)}, u32[]{:S(2)}) copy-start(s32[32]{0:T(128)} %param.6) | copy-start | bytes 388
  7.2 28.7 %copy-start.1 = (bf16[4,2,128,128]{3,2,1,0:T(8,128)(2,1)S(1)}, bf16[4,2,128,128]{3,2,1,0:T(8,128)(2,1)}, u32[]{:S(2)}) copy-start(bf16[4,2,128,128]{3,2,1,0:T(8,128)(2,1)} %param.5) | copy-start | bytes 786436
  7.2 284.8 %all-to-all-start = ((bf16[8,2,4,32,2,128]{5,4,3,2,1,0:T(2,128)(2,1)}), bf16[8,2,4,32,2,128]{5,4,3,2,1,0:T(2,128)(2,1)S(1)}, u32[]{:S(2)}, u32[]{:S(2)}) async-start(bf16[8,2,4,32,2,128]{5,4,3,2,1,0:T(2,128)(2,1)} %param.4), calls=%async_computation | async-start | bytes 2097152 | tf_op jit(solution)/shard_map/all_to_all | solution.py:47
  11.6 371.2 %reduce-scatter.2.cloned.1.call-start = ((), (), s32[]{:S(2)}) async-start(), calls=%async_computation.3 | async-start | bytes 589824 | tf_op jit(solution)/shard_map/reduce_scatter | solution.py:76
  318.2 65.6 %copy-start.2 = (s32[8,4096]{1,0:T(8,128)S(1)}, s32[8,4096]{1,0:T(8,128)}, u32[]{:S(2)}) copy-start(s32[8,4096]{1,0:T(8,128)} %param.7) | copy-start | bytes 393220
  319.1 244.9 %all-reduce.2.cloned.1.call-start = ((), (), s32[]{:S(2)}) async-start(), calls=%async_computation.4 | async-start | bytes 262144 | tf_op jit(solution)/shard_map/psum | solution.py:112
  424.2 16.2 %copy-start = (bf16[4,32,2,128]{3,1,2,0:T(8,128)(2,1)S(1)}, bf16[4,32,2,128]{3,1,2,0:T(8,128)(2,1)}, u32[]{:S(2)}) copy-start(bf16[4,32,2,128]{3,1,2,0:T(8,128)(2,1)} %reduce-scatter.2.cloned.1.call-done) | copy-start | bytes 196612
Sparse Core Ops, SparseCore 0:
  319.2 63.5 reduce-scatter.1
  440.5 123.4 all-reduce.1
